TPU v7x, 32 devices: a whole 2x2x4 slice. The times are simulated.
32 devices in a mesh: lat: 8 (over z, x), lev: 4 (over y, core).
Axes of the slice: x: 2, y: 2, z: 4, core: 2. Of those that a mesh axis runs over, the one named last changes fastest.
Arguments:
- grid: bfloat16 [640, 128, 4, 1280], P('lat', 'lev'), may hold values from -6 to 6
- legendre: bfloat16 [640, 640, 640], P('lat'), may hold values from -0.25 to 0.25
- vertical: bfloat16 [128, 128], P('lev'), may hold values from -0.5 to 0.5
- damping: bfloat16 [128], P('lev'), may hold values from 1 to 16
- lon_counts: int32 [640], replicated, may hold values from 160 to 1280
- wave_slots: int32 [640], replicated, may hold values from 0 to 639, as said below
Outputs:
- filtered_grid: bfloat16 [640, 128, 4, 1280], P('lat', 'lev')
Inputs may be any that keep to these rules, and one draw needn't show every extreme that they name: wave_slots is a permutation; slot g * 20 + r holds a wavenumber from r * 32 to (r + 1) * 32 - 1.
All inputs are finite; a program needn't handle non-finite values.
Results may differ from a plain program's by a relative error of at most 0.0074.
Values may be sent and summed in bfloat16 or wider, within the bound.
A program may use at most 512 MiB of HBM per device.

v0:
```python
import math

import jax
import jax.numpy as jnp
from jax import lax
from jax.sharding import PartitionSpec as P


def forward_build(wavenumbers, longitudes):
    points = jnp.arange(longitudes, dtype=jnp.int32)
    phase = (wavenumbers[:, None] * points[None, :] % longitudes).astype(jnp.float32) * (
        2.0 * math.pi / longitudes
    )
    scale = 1.0 / math.sqrt(longitudes)
    return jnp.stack([jnp.cos(phase) * scale, -jnp.sin(phase) * scale], axis=1).astype(jnp.bfloat16)


def inverse_build(wavenumbers, longitudes):
    points = jnp.arange(longitudes, dtype=jnp.int32)
    phase = (wavenumbers[:, None] * points[None, :] % longitudes).astype(jnp.float32) * (
        2.0 * math.pi / longitudes
    )
    scale = 1.0 / math.sqrt(longitudes)
    weight = jnp.where(wavenumbers == 0, 1.0, 2.0).astype(jnp.float32)[:, None]
    return jnp.stack(
        [jnp.cos(phase) * scale * weight, -jnp.sin(phase) * scale * weight], axis=1
    ).astype(jnp.bfloat16)


def damping_factor(degrees, damping):
    degree_values = jnp.arange(degrees).astype(jnp.float32)
    ratio = degree_values * (degree_values + 1.0) / float(degrees * (degrees - 1))
    return 1.0 / (1.0 + damping.astype(jnp.float32)[None, :] * (ratio * ratio)[:, None])


def legendre_forward(table, fourier, wavenumbers):
    degrees = table.shape[1]
    spectral = jnp.einsum("sna,srac->snrc", table, fourier, preferred_element_type=jnp.float32)
    live = (jnp.arange(degrees, dtype=jnp.int32)[None, :] >= wavenumbers[:, None]).astype(
        jnp.float32
    )
    return (spectral * live[:, :, None, None]).astype(jnp.bfloat16)


def legendre_inverse(table, mixed):
    banded = jnp.einsum("sna,snrc->srac", table, mixed, preferred_element_type=jnp.float32)
    return banded.astype(jnp.bfloat16)


def per_device(grid, legendre, vertical, damping, lon_counts, wave_slots):
    lat_rows, level_rows, fields, longitudes = grid.shape
    slot_count = wave_slots.shape[0]
    degrees = legendre.shape[1]
    forward_table = forward_build(wave_slots, longitudes)
    own_counts = lax.dynamic_slice_in_dim(lon_counts, lax.axis_index("lat") * lat_rows, lat_rows)
    fourier = jnp.einsum("mrx,alfx->mralf", forward_table, grid, preferred_element_type=jnp.float32)
    fourier = fourier.reshape(slot_count, 2, lat_rows, level_rows * fields)
    forward_kept = (2 * wave_slots[:, None] < own_counts[None, :]).astype(jnp.float32)
    fourier = (fourier * forward_kept[:, None, :, None]).astype(jnp.bfloat16)
    gathered = lax.all_to_all(fourier, "lat", split_axis=0, concat_axis=2, tiled=True)
    count = gathered.shape[0]
    own_waves = lax.dynamic_slice_in_dim(wave_slots, lax.axis_index("lat") * count, count)
    spectral = legendre_forward(legendre, gathered, own_waves)
    piece = lax.all_gather(spectral, "lev", axis=3, tiled=True)
    level_count = piece.shape[3] // fields
    block = piece.reshape(piece.shape[0], piece.shape[1], 2, level_count, fields)
    folded = jnp.einsum("snrkf,lk->snrlf", block, vertical, preferred_element_type=jnp.float32)
    own_part = spectral.reshape(count, degrees, 2, level_rows, fields).astype(jnp.float32)
    mixed = (own_part + folded) * damping_factor(degrees, damping)[None, :, None, :, None]
    mixed = mixed.astype(jnp.bfloat16).reshape(count, degrees, 2, level_rows * fields)
    banded = legendre_inverse(legendre, mixed)
    returned = lax.all_to_all(banded, "lat", split_axis=2, concat_axis=0, tiled=True)
    inverse_table = inverse_build(wave_slots, longitudes)
    back_kept = (2 * wave_slots[:, None] < own_counts[None, :]).astype(jnp.bfloat16)
    returned = returned * back_kept[:, None, :, None]
    filtered_grid = jnp.einsum(
        "mrac,mrx->acx", returned, inverse_table, preferred_element_type=jnp.float32
    )
    return filtered_grid.reshape(lat_rows, level_rows, fields, longitudes).astype(jnp.bfloat16)


def solution(mesh):
    return jax.shard_map(
        per_device,
        mesh=mesh,
        in_specs=(
            P("lat", "lev", None, None),
            P("lat", None, None),
            P("lev", None),
            P("lev"),
            P(),
            P(),
        ),
        out_specs=P("lat", "lev", None, None),
        check_vma=False,
    )
```

profile of v0, /device:TPU:0, one launch (start us, length us, event | category | flops | bytes accessed | tf_op | source)
XLA Modules:
  0.0 2570.0 jit_solution(2957762633101189925)
XLA Ops:
  6.5 0.0 copy-start
  6.5 0.7 broadcast_multiply_fusion
  7.2 0.7 select_multiply_fusion
  7.9 17.2 multiply_convert_fusion.3
  25.1 55.3 %fusion.9 = f32[640,2,80,32,4]{0,2,4,3,1:T(8,128)} fusion(bf16[80,32,4,1280]{3,2,1,0:T(4,128)(2,1)} %param.6, bf16[640,1,1280]{2,0,1:T(8,128)(2,1)S(1)} %get-tuple-element.9, bf16[640,1,1280]{2,0,1:T(8,128)(2,1)S(1)} %get-tuple-element.10), kind=kOutput, calls=%fused_computation.14 | convolution fusion | flops 33560985600 | bytes 81920000 | tf_op jit(solution)/shard_map/mrx,alfx->mralf/dot_general | solution.py:56
  80.4 58.4 %copy.27 = f32[640,2,80,128]{3,2,1,0:T(8,128)} copy(f32[640,2,80,128]{0,2,3,1:T(8,128)} %bitcast.69) | data formatting | bytes 104857600 | tf_op jit(solution)/shard_map/reshape | solution.py:57
  138.9 0.8 dynamic_slice.6
  139.6 0.8 compare_convert_fusion
  140.4 26.3 %multiply_convert_fusion.1 = bf16[640,2,80,128]{3,2,1,0:T(8,128)(2,1)} fusion(f32[640,2,80,128]{3,2,1,0:T(8,128)} %copy.27, f32[640,80]{1,0:T(8,128)S(1)} %get-tuple-element.8), kind=kLoop, calls=%fused_computation.11 | loop fusion | flops 26214400 | bytes 78848000 | tf_op jit(solution)/shard_map/convert_element_type | solution.py:59
  166.7 18.2 all-to-all-start
  184.9 0.0 all-gather.2.cloned.1.call-start
  185.0 0.8 dynamic_slice.7
  185.7 0.1 fusion.32
  185.8 565.9 %all-to-all-done = bf16[640,2,80,128]{3,2,1,0:T(8,128)(2,1)} async-done(((bf16[640,2,80,128]{3,2,1,0:T(8,128)(2,1)}), bf16[640,2,80,128]{3,2,1,0:T(8,128)(2,1)}, u32[]{:S(2)}, u32[]{:S(2)}) %all-to-all-start) | async-done | bytes 26214432 | tf_op jit(solution)/shard_map/all_to_all | solution.py:60
  751.8 21.8 copy.28
  773.6 42.9 %fusion.8 = bf16[80,640,2,128]{1,3,2,0:T(8,128)(2,1)} fusion(f32[80,640]{1,0:T(8,128)S(1)} %fusion.32, bf16[80,2,640,128]{3,2,1,0:T(8,128)(2,1)} %bitcast.71, bf16[80,640,640]{2,1,0:T(8,128)(2,1)} %param.7), kind=kOutput, calls=%fused_computation.12 | convolution fusion | flops 16803430400 | bytes 118169600 | tf_op jit(solution)/shard_map/sna,srac->snrc/dot_general | solution.py:38
  816.5 0.0 copy-start.5
  816.5 0.0 all-gather.2.cloned.1.call-update
  816.6 0.6 copy-done.5
  817.2 0.1 add_divide_fusion
  817.3 50.3 %reshape.290 = f32[80,640,2,32,4]{1,4,3,2,0:T(4,128)} reshape(bf16[80,640,2,128]{1,3,2,0:T(8,128)(2,1)} %fusion.8) | data formatting | bytes 78643200 | tf_op jit(solution)/shard_map/convert_element_type | solution.py:68
  867.6 557.3 %all-gather.2.cloned.1.call-done = bf16[80,640,2,512]{1,3,2,0:T(8,128)(2,1)} async-done(((bf16[80,640,2,128]{1,3,2,0:T(8,128)(2,1)}), bf16[80,640,2,512]{1,3,2,0:T(8,128)(2,1)}) %all-gather.2.cloned.1.call-update) | async-done | bytes 104857616 | tf_op jit(solution)/shard_map/all_gather | solution.py:64
  1424.9 168.4 %reshape.288 = bf16[80,640,2,128,4]{1,4,3,2,0:T(4,128)(2,1)} reshape(bf16[80,640,2,512]{1,3,2,0:T(8,128)(2,1)} %all-gather.2.cloned.1.call-done) | data formatting | bytes 209715200 | tf_op jit(solution)/shard_map/reshape | solution.py:66
  1593.3 0.0 copy-done
  1593.3 64.9 %fusion.7 = bf16[80,640,2,32,4]{1,3,4,2,0:T(8,128)(2,1)} fusion(f32[80,640,2,32,4]{1,4,3,2,0:T(4,128)} %reshape.290, f32[640,32]{0,1:T(8,128)S(1)} %add_divide_fusion, bf16[80,640,2,128,4]{1,4,3,2,0:T(4,128)(2,1)} %reshape.288, bf16[32,128]{1,0:T(8,128)(2,1)S(1)} %copy-done), kind=kOutput, calls=%fused_computation.9 | convolution fusion | flops 3394764800 | bytes 183590912 | tf_op jit(solution)/shard_map/snrkf,lk->snrlf/dot_general | solution.py:67
  1658.2 18.6 copy.32
  1676.8 54.9 %convert_bitcast_fusion = bf16[80,2,640,128]{2,3,1,0:T(8,128)(2,1)} fusion(bf16[80,640,640]{2,1,0:T(8,128)(2,1)} %param.7, bf16[80,640,2,128]{1,0,3,2:T(8,128)(2,1)} %bitcast.72), kind=kOutput, calls=%fused_computation.19 | convolution fusion | flops 16790323200 | bytes 117964800 | tf_op jit(solution)/shard_map/sna,snrc->srac/dot_general | solution.py:46
  1731.7 64.2 %copy.34 = bf16[80,2,640,128]{3,1,0,2:T(2,128)(2,1)} copy(bf16[80,2,640,128]{2,3,1,0:T(8,128)(2,1)} %convert_bitcast_fusion) | data formatting | bytes 52428800 | tf_op jit(solution)/shard_map/convert_element_type | solution.py:47
  1795.9 570.9 %all_to_all.36 = bf16[80,2,640,128]{3,1,0,2:T(2,128)(2,1)S(1)} all-to-all(bf16[80,2,640,128]{3,1,0,2:T(2,128)(2,1)} %copy.34), channel_id=1, replica_groups=mesh['lat'=8,'lev'=4] {'lat'}, dimensions={2} | all-to-all | bytes 52428800 | tf_op jit(solution)/shard_map/all_to_all | solution.py:72
  2366.9 12.7 copy.35
  2379.6 0.0 copy-start.4
  2379.6 21.3 copy.36
  2400.8 0.0 copy-done.4
  2400.8 18.0 bitcast_multiply_fusion
  2418.8 0.0 copy-start.2
  2418.8 0.0 copy-start.3
  2418.8 42.8 %copy.37 = bf16[80,128,640,2]{2,0,3,1:T(8,128)(2,1)} copy(bf16[80,128,640,2]{1,0,3,2:T(8,128)(2,1)} %bitcast.67) | data formatting | bytes 52428800 | tf_op jit(solution)/shard_map/mrac,mrx->acx/dot_general | solution.py:76
  2461.6 0.0 copy-done.2
  2461.6 0.0 copy-done.3
  2461.6 0.0 copy-start.1
  2461.7 71.1 %bitcast_convert_fusion = bf16[80,32,4,1280]{3,1,2,0:T(8,128)(2,1)} fusion(bf16[80,32,4,640,2]{3,0,4,2,1:T(8,128)(2,1)} %bitcast.70, bf16[640,1,1280]{2,0,1:T(8,128)(2,1)S(1)} %copy-done.3, bf16[640,1,1280]{2,0,1:T(8,128)(2,1)S(1)} %copy-done.2), kind=kOutput, calls=%fused_computation.6 | convolution fusion | flops 33569177600 | bytes 55705600 | tf_op jit(solution)/shard_map/mrac,mrx->acx/dot_general | solution.py:76
  2532.8 29.9 %copy.39 = bf16[80,32,4,1280]{3,2,1,0:T(4,128)(2,1)} copy(bf16[80,32,4,1280]{3,1,2,0:T(8,128)(2,1)} %bitcast_convert_fusion) | data formatting | bytes 52428800 | tf_op jit(solution)/shard_map/convert_element_type | solution.py:79
  2562.7 0.0 copy-done.1
  (2 shorter events, 0.0 us)
Async XLA Ops:
  6.5 1586.7 %copy-start = (bf16[32,128]{1,0:T(8,128)(2,1)S(1)}, bf16[32,128]{1,0:T(8,128)(2,1)}, u32[]{:S(2)}) copy-start(bf16[32,128]{1,0:T(8,128)(2,1)} %param.8) | copy-start | bytes 24580
  166.7 585.0 %all-to-all-start = ((bf16[640,2,80,128]{3,2,1,0:T(8,128)(2,1)}), bf16[640,2,80,128]{3,2,1,0:T(8,128)(2,1)}, u32[]{:S(2)}, u32[]{:S(2)}) async-start(bf16[640,2,80,128]{3,2,1,0:T(8,128)(2,1)} %multiply_convert_fusion.1), calls=%async_computation | async-start | bytes 52428800 | tf_op jit(solution)/shard_map/all_to_all | solution.py:60
  184.9 1240.0 %all-gather.2.cloned.1.call-start = ((), (), s32[]{:S(2)}) async-start(), calls=%async_computation.2 | async-start | bytes 131072000 | tf_op jit(solution)/shard_map/all_gather | solution.py:64
  816.5 0.7 copy-start.5
  2379.6 21.3 copy-start.4
  2418.8 42.8 %copy-start.2 = (bf16[640,1,1280]{2,0,1:T(8,128)(2,1)S(1)}, bf16[640,1,1280]{2,0,1:T(8,128)(2,1)}, u32[]{:S(2)}) copy-start(bf16[640,1,1280]{2,0,1:T(8,128)(2,1)} %get-tuple-element.5) | copy-start | bytes 4915204
  2418.8 42.9 %copy-start.3 = (bf16[640,1,1280]{2,0,1:T(8,128)(2,1)S(1)}, bf16[640,1,1280]{2,0,1:T(8,128)(2,1)}, u32[]{:S(2)}) copy-start(bf16[640,1,1280]{2,0,1:T(8,128)(2,1)} %get-tuple-element.6) | copy-start | bytes 4915204
  2461.6 101.1 %copy-start.1 = (bf16[32,128]{1,0:T(8,128)(2,1)S(1)}, bf16[32,128]{1,0:T(8,128)(2,1)}, u32[]{:S(2)}) copy-start(bf16[32,128]{1,0:T(8,128)(2,1)} %param.8) | copy-start | bytes 24580
Sparse Core Ops, SparseCore 0:
  816.7 608.1 all-gather.1
where the time goes:
time: 2590 us; the launch traced here: 2570 us
  waiting for transfers between devices  1120 us (43%)
  blocking collectives  571 us (22%)
  local copies, waits for them, and re-layouts  491 us (19%)
  matrix products  289 us (11%)
  other arithmetic  63.8 us (2%)
    all_to_all x1, blocking collectives, per_device(): lax.all_to_all(banded, 'lat', split_axis=2, concat_axis=0, tiled=True)  571 us
    all_to_all x1, waiting for transfers between devices, per_device(): lax.all_to_all(fourier, 'lat', split_axis=0, concat_axis=2, tiled=True)  566 us
    all_gather x1, waiting for transfers between devices, per_device(): piece = lax.all_gather(spectral, 'lev', axis=3, tiled=True)  557 us
    reshape x1, local copies, waits for them, and re-layouts, per_device(): piece.reshape(piece.shape[0], piece.shape[1], 2, level_count, fields)  168 us
    dot_general x1, matrix products, per_device(): jnp.einsum('mrac,mrx->acx', returned, inverse_table, preferred_element_ty...  71.1 us
    dot_general x1, matrix products, per_device(): jnp.einsum('snrkf,lk->snrlf', block, vertical, preferred_element_type=jnp...  64.9 us
    convert_element_type x1, local copies, waits for them, and re-layouts, legendre_inverse(): return banded.astype(jnp.bfloat16)  64.2 us
    reshape x1, local copies, waits for them, and re-layouts, per_device(): fourier = fourier.reshape(slot_count, 2, lat_rows, level_rows * fields)  58.4 us
  transfers between devices with their start and end apart: 2, of which 2 were waited for; matrix products, arithmetic and copies ran while one was open for 2% of the time, Pallas kernels for 0%

commit v1 on v0

v1 whole, which is shorter than its diff:
```python
import functools
import math

import jax
import jax.numpy as jnp
from jax import lax
from jax.experimental import pallas as pl
from jax.experimental.pallas import tpu as pltpu
from jax.sharding import PartitionSpec as P

CHUNKS = 4
VMEM_LIMIT = 60 * 1024 * 1024


def table_build(wavenumbers, longitudes):
    points = jnp.arange(longitudes, dtype=jnp.int32)
    phase = (wavenumbers[:, None] * points[None, :] % longitudes).astype(jnp.float32) * (
        2.0 * math.pi / longitudes
    )
    scale = 1.0 / math.sqrt(longitudes)
    return jnp.concatenate([jnp.cos(phase) * scale, -jnp.sin(phase) * scale], axis=0).astype(
        jnp.bfloat16
    )


def row_block(rows):
    return 16 if rows % 16 == 0 else rows


def forward_body(block, padded, cols, lon_ref, grid_ref, table_ref, wave_ref, out_ref, held):
    base = pl.program_id(0) * block
    both = table_ref.shape[0]
    step = 2 if block % 2 == 0 else 1
    for row in range(0, block, step):
        points = grid_ref[row : row + step].reshape(step * cols, grid_ref.shape[2])
        result = lax.dot_general(
            table_ref[...], points, (((1,), (1,)), ((), ())), preferred_element_type=jnp.float32
        )
        for part in range(step):
            keep = 2 * wave_ref[...] < lon_ref[base + row + part]
            piece = result[:, part * cols : (part + 1) * cols]
            held[pl.ds(row + part, both, stride=padded), :] = jnp.where(keep, piece, 0.0)
    half = both // 2
    full = held[...].reshape(2, half, padded, cols)
    for part in range(2):
        out_ref[:, part] = full[part, :, :block].astype(out_ref.dtype)


def forward_fourier(grid, table, waves, counts):
    rows, cols, longitudes = grid.shape
    both = table.shape[0]
    block = row_block(rows)
    padded = -(-block // 8) * 8
    return pl.pallas_call(
        functools.partial(forward_body, block, padded, cols),
        out_shape=jax.ShapeDtypeStruct((both // 2, 2, rows, cols), jnp.bfloat16),
        grid_spec=pltpu.PrefetchScalarGridSpec(
            num_scalar_prefetch=1,
            grid=(rows // block,),
            in_specs=[
                pl.BlockSpec((block, cols, longitudes), lambda i, c: (i, 0, 0)),
                pl.BlockSpec((both, longitudes), lambda i, c: (0, 0)),
                pl.BlockSpec((both, cols), lambda i, c: (0, 0)),
            ],
            out_specs=pl.BlockSpec((both // 2, 2, block, cols), lambda i, c: (0, 0, i, 0)),
            scratch_shapes=[pltpu.VMEM((both * padded, cols), jnp.float32)],
        ),
        compiler_params=pltpu.CompilerParams(vmem_limit_bytes=VMEM_LIMIT),
        cost_estimate=pl.CostEstimate(
            flops=2 * both * rows * cols * longitudes,
            bytes_accessed=2 * rows * cols * (longitudes + both),
            transcendentals=0,
        ),
        name="forward_fourier",
    )(counts, grid, table, waves)


def spectral_body(lat_size, lev_size, rows, cols, own_ref, wave_ref, table_ref, in_ref, mixer_ref, factor_ref, out_ref):
    table = table_ref[0]
    degrees = table.shape[0]
    width = lev_size * cols
    wave = wave_ref[pl.program_id(0)]
    live = lax.broadcasted_iota(jnp.int32, (degrees, width), 0) >= wave
    for part in range(2):
        fourier = jnp.concatenate(
            [
                jnp.concatenate(
                    [in_ref[i * lev_size + j, 0, part] for i in range(lat_size)], axis=0
                )
                for j in range(lev_size)
            ],
            axis=1,
        )
        spectral = jnp.dot(table, fourier, preferred_element_type=jnp.float32)
        spectral = jnp.where(live, spectral, 0.0).astype(jnp.bfloat16)
        folded = jnp.dot(spectral, mixer_ref[...], preferred_element_type=jnp.float32)
        mixed = ((spectral.astype(jnp.float32) + folded) * factor_ref[...]).astype(jnp.bfloat16)
        banded = lax.dot_general(
            table, mixed, (((0,), (0,)), ((), ())), preferred_element_type=jnp.float32
        ).astype(jnp.bfloat16)
        for i in range(lat_size):
            for j in range(lev_size):
                out_ref[i * lev_size + j, 0, part] = banded[
                    i * rows : (i + 1) * rows, j * cols : (j + 1) * cols
                ]


def spectral_step(legendre, gathered, mixer, factor, first_slot, own_waves, lat_size, lev_size):
    owners, count, _, rows, cols = gathered.shape
    degrees, latitudes = legendre.shape[1:]
    width = lev_size * cols
    block = pl.BlockSpec((owners, 1, 2, rows, cols), lambda s, o, w: (0, s, 0, 0, 0))
    return pl.pallas_call(
        functools.partial(spectral_body, lat_size, lev_size, rows, cols),
        out_shape=jax.ShapeDtypeStruct(gathered.shape, jnp.bfloat16),
        grid_spec=pltpu.PrefetchScalarGridSpec(
            num_scalar_prefetch=2,
            grid=(count,),
            in_specs=[
                pl.BlockSpec((1, degrees, latitudes), lambda s, o, w: (o[0] + s, 0, 0)),
                block,
                pl.BlockSpec((width, width), lambda s, o, w: (0, 0)),
                pl.BlockSpec((degrees, width), lambda s, o, w: (0, 0)),
            ],
            out_specs=block,
        ),
        compiler_params=pltpu.CompilerParams(vmem_limit_bytes=VMEM_LIMIT),
        cost_estimate=pl.CostEstimate(
            flops=count * 4 * degrees * width * (2 * latitudes + width),
            bytes_accessed=2 * count * degrees * latitudes + 4 * gathered.size,
            transcendentals=0,
        ),
        name="spectral_step",
    )(first_slot, own_waves, legendre, gathered, mixer, factor)


def inverse_body(count, block, padded, cols, carried, lon_ref, *refs):
    pieces, tables, waves = refs[:count], refs[count : 2 * count], refs[2 * count : 3 * count]
    before = refs[3 * count] if carried else None
    out_ref = refs[3 * count + (1 if carried else 0)]
    helds = refs[3 * count + (2 if carried else 1) :]
    base = pl.program_id(0) * block
    step = 2 if block % 2 == 0 else 1
    for piece, held in zip(pieces, helds):
        half = piece.shape[0]
        for part in range(2):
            value = piece[:, part].astype(jnp.float32)
            if padded != block:
                value = jnp.pad(value, ((0, 0), (0, padded - block), (0, 0)))
            span = half * padded
            held[part * span : (part + 1) * span, :] = value.reshape(span, cols)
    for row in range(0, block, step):
        total = None
        for held, table, wave in zip(helds, tables, waves):
            both = table.shape[0]
            weight = jnp.where(wave[...] == 0, 1.0, 2.0)
            columns = []
            for part in range(step):
                keep = 2 * wave[...] < lon_ref[base + row + part]
                value = held[pl.ds(row + part, both, stride=padded), :]
                columns.append(jnp.where(keep, value * weight, 0.0).astype(jnp.bfloat16))
            banded = jnp.concatenate(columns, axis=1) if step > 1 else columns[0]
            product = lax.dot_general(
                banded, table[...], (((0,), (0,)), ((), ())), preferred_element_type=jnp.float32
            )
            total = product if total is None else total + product
        total = total.reshape(step, cols, total.shape[1])
        if carried:
            total = total + before[row : row + step]
        out_ref[row : row + step] = total.astype(out_ref.dtype)


def inverse_fourier(pieces, tables, waves, counts, before, kind):
    rows, cols = pieces[0].shape[2:]
    longitudes = tables[0].shape[1]
    block = row_block(rows)
    if block == 16:
        block = 8 if before is None and kind == jnp.float32 or before is not None else 16
    block = 16 if rows % 16 == 0 else rows
    padded = -(-block // 8) * 8
    carried = before is not None
    grid_block = pl.BlockSpec((block, cols, longitudes), lambda i, c: (i, 0, 0))
    in_specs = (
        [pl.BlockSpec((p.shape[0], 2, block, cols), lambda i, c: (0, 0, i, 0)) for p in pieces]
        + [pl.BlockSpec(t.shape, lambda i, c: (0, 0)) for t in tables]
        + [pl.BlockSpec(w.shape, lambda i, c: (0, 0)) for w in waves]
        + ([grid_block] if carried else [])
    )
    total = sum(t.shape[0] for t in tables)
    return pl.pallas_call(
        functools.partial(inverse_body, len(pieces), block, padded, cols, carried),
        out_shape=jax.ShapeDtypeStruct((rows, cols, longitudes), kind),
        grid_spec=pltpu.PrefetchScalarGridSpec(
            num_scalar_prefetch=1,
            grid=(rows // block,),
            in_specs=in_specs,
            out_specs=grid_block,
            scratch_shapes=[
                pltpu.VMEM((t.shape[0] * padded, cols), jnp.float32) for t in tables
            ],
        ),
        compiler_params=pltpu.CompilerParams(vmem_limit_bytes=VMEM_LIMIT),
        cost_estimate=pl.CostEstimate(
            flops=2 * total * rows * cols * longitudes,
            bytes_accessed=rows * cols * (2 * total + 4 * longitudes),
            transcendentals=0,
        ),
        name="inverse_fourier",
    )(counts, *pieces, *tables, *waves, *([before] if carried else []))


def per_device(lat_size, lev_size, grid, legendre, vertical, damping, lon_counts, wave_slots):
    lat_rows, level_rows, fields, longitudes = grid.shape
    cols = level_rows * fields
    owners = lat_size * lev_size
    rounds = wave_slots.shape[0] // owners
    degrees = legendre.shape[1]
    axes = ("lat", "lev")
    lat, lev = lax.axis_index("lat"), lax.axis_index("lev")
    counts = lax.dynamic_slice_in_dim(lon_counts, lat * lat_rows, lat_rows)
    owner_waves = wave_slots.reshape(owners, rounds)
    own_waves = lax.dynamic_slice_in_dim(wave_slots, (lat * lev_size + lev) * rounds, rounds)

    coupling = lax.all_gather(vertical, "lev", axis=0, tiled=True)
    strength = lax.all_gather(damping, "lev", axis=0, tiled=True)
    mixer = jnp.kron(coupling.T, jnp.eye(fields, dtype=coupling.dtype))
    degree_values = jnp.arange(degrees).astype(jnp.float32)
    ratio = degree_values * (degree_values + 1.0) / float(degrees * (degrees - 1))
    lanes = jnp.repeat(strength.astype(jnp.float32), fields)
    factor = 1.0 / (1.0 + lanes[None, :] * (ratio * ratio)[:, None])

    points = grid.reshape(lat_rows, cols, longitudes)
    chunk_count = min(CHUNKS, rounds)
    edges = [rounds * c // chunk_count for c in range(chunk_count + 1)]
    tables, waves, returned = [], [], []
    for low, high in zip(edges[:-1], edges[1:]):
        count = high - low
        slots = owner_waves[:, low:high].reshape(-1)
        table = table_build(slots, longitudes)
        wave = jnp.broadcast_to(jnp.tile(slots, 2)[:, None], (2 * slots.shape[0], cols))
        fourier = forward_fourier(points, table, wave, counts)
        fourier = fourier.reshape(owners, count, 2, lat_rows, cols)
        gathered = lax.all_to_all(fourier, axes, split_axis=0, concat_axis=0, tiled=True)
        banded = spectral_step(
            legendre,
            gathered,
            mixer,
            factor,
            (lev * rounds + low).reshape(1),
            own_waves[low:high],
            lat_size,
            lev_size,
        )
        back = lax.all_to_all(banded, axes, split_axis=0, concat_axis=0, tiled=True)
        tables.append(table)
        waves.append(wave)
        returned.append(back.reshape(owners * count, 2, lat_rows, cols))
    before = None
    if chunk_count > 1:
        for c in range(chunk_count - 1):
            before = inverse_fourier(
                returned[c : c + 1], tables[c : c + 1], waves[c : c + 1], counts, before, jnp.float32
            )
    filtered = inverse_fourier(
        returned[-1:], tables[-1:], waves[-1:], counts, before, jnp.bfloat16
    )
    return filtered.reshape(lat_rows, level_rows, fields, longitudes)


def solution(mesh):
    return jax.shard_map(
        functools.partial(per_device, mesh.shape["lat"], mesh.shape["lev"]),
        mesh=mesh,
        in_specs=(
            P("lat", "lev", None, None),
            P("lat", None, None),
            P("lev", None),
            P("lev"),
            P(),
            P(),
        ),
        out_specs=P("lat", "lev", None, None),
        check_vma=False,
    )
```

time: 2590 us -> 1370 us (0.53)
  blocking collectives: 571 us -> 45.6 us
  local copies, waits for them, and re-layouts: 491 us -> 126 us
  waiting for transfers between devices: 1120 us -> 816 us
  Pallas kernels: 0 us -> 295 us
  matrix products: 289 us -> 0 us
  other arithmetic: 63.8 us -> 26.4 us
  starting transfers between devices: 18.2 us -> 50.5 us
    all_to_all x1 -> x0, blocking collectives: 571 us -> none  [per_device(): lax.all_to_all(banded, 'lat', split_axis=2, concat_axis=0, tiled=True)]
    all_gather x1 -> x0, waiting for transfers between devices: 557 us -> none  [per_device(): piece = lax.all_gather(spectral, 'lev', axis=3, tiled=True)]
    pallas_call x0 -> x12, Pallas kernels: none -> 295 us  [the longest x4 148 us: inverse_fourier(): pl.pallas_call(functools.partial(inverse_body, len(pieces), block, padded...]
    dot_general x5 -> x0, matrix products: 289 us -> none  [the longest x1 71.1 us: per_device(): jnp.einsum('mrac,mrx->acx', returned, inverse_table, preferred_element_ty...]
    all_to_all x1 -> x8, waiting for transfers between devices: 566 us -> 816 us  [the longest x4 413 us: per_device(): back = lax.all_to_all(banded, axes, split_axis=0, concat_axis=0, tiled=True)]
    convert_element_type x4 -> x0, local copies, waits for them, and re-layouts: 163 us -> none  [the longest x1 64.2 us: legendre_inverse(): return banded.astype(jnp.bfloat16)]
    reshape x2 -> x3, local copies, waits for them, and re-layouts: 227 us -> 84.7 us  [the longest x1 42.9 us: per_device(): return filtered.reshape(lat_rows, level_rows, fields, longitudes)]
    all_to_all x3 -> x0, local copies, waits for them, and re-layouts: 55.8 us -> none  [the longest x2 34 us: per_device(): lax.all_to_all(banded, 'lat', split_axis=2, concat_axis=0, tiled=True)]
  transfers between devices with their start and end apart: 2 -> 8, of which waited for: 2 -> 8; matrix products, arithmetic and copies ran while one was open for 2% -> 4% of each run, Pallas kernels for 0% -> 18%
where the time goes in v1:
time: 1370 us; the launch traced here: 1360 us
  waiting for transfers between devices  816 us (60%)
  Pallas kernels  295 us (22%)
  local copies, waits for them, and re-layouts  126 us (9%)
  starting transfers between devices  50.5 us (4%)
  blocking collectives  45.6 us (3%)
  other arithmetic  26.4 us (2%)
    all_to_all x4, waiting for transfers between devices, per_device(): back = lax.all_to_all(banded, axes, split_axis=0, concat_axis=0, tiled=True)  413 us
    all_to_all x4, waiting for transfers between devices, per_device(): lax.all_to_all(fourier, axes, split_axis=0, concat_axis=0, tiled=True)  403 us
    pallas_call x4, Pallas kernels, inverse_fourier(): pl.pallas_call(functools.partial(inverse_body, len(pieces), block, padded...  148 us
    pallas_call x4, Pallas kernels, spectral_step(): pl.pallas_call(functools.partial(spectral_body, lat_size, lev_size, rows,...  75.4 us
    pallas_call x4, Pallas kernels, forward_fourier(): pl.pallas_call(functools.partial(forward_body, block, padded, cols), out_...  71.9 us
    reshape x1, local copies, waits for them, and re-layouts, per_device(): return filtered.reshape(lat_rows, level_rows, fields, longitudes)  42.9 us
    reshape x1, local copies, waits for them, and re-layouts, per_device(): points = grid.reshape(lat_rows, cols, longitudes)  41 us
    all_gather x1, blocking collectives, per_device(): coupling = lax.all_gather(vertical, 'lev', axis=0, tiled=True)  37.4 us
  transfers between devices with their start and end apart: 8, of which 8 were waited for; matrix products, arithmetic and copies ran while one was open for 4% of the time, Pallas kernels for 18%

profile of v1, /device:TPU:0, one launch (start us, length us, event | category | flops | bytes accessed | tf_op | source)
XLA Modules:
  0.0 1361.3 jit_solution(14778676394348641290)
XLA Ops:
  0.0 0.8 reshape.82
  1.0 3.8 multiply_convert_fusion.1
  4.8 41.0 %reshape.81.grid_ref = bf16[80,128,1280]{2,1,0:T(8,128)(2,1)} reshape(bf16[80,32,4,1280]{3,2,1,0:T(4,128)(2,1)} %param.6) | data formatting | bytes 52428800 | tf_op jit(solution)/shard_map/reshape | solution.py:232
  45.9 1.3 dynamic_slice.6.lon_ref
  47.2 1.0 pad_maximum_fusion.3.table_ref.refs_1_
  48.1 0.8 broadcast_in_dim.48.wave_ref.refs_2_
  48.9 18.0 %forward_fourier.7 = bf16[160,2,80,128]{3,2,1,0:T(8,128)(2,1)} custom-call(s32[80]{0:T(128)} %dynamic_slice.6.lon_ref, bf16[80,128,1280]{2,1,0:T(8,128)(2,1)} %reshape.81.grid_ref, bf16[320,1280]{1,0:T(8,128)(2,1)} %pad_maximum_fusion.3.table_ref.refs_1_, s32[320,128]{1,0:T(8,128)} %broadcast_in_dim.48.wave_ref.refs_2_), custom_call_target="tpu_custom_call" | custom-call | flops 8388608000 | bytes 32768000 | tf_op jit(solution)/shard_map/forward_fourier/pallas_call | solution.py:54
  66.9 7.4 all-to-all-start.6
  74.6 3.7 multiply_convert_fusion.3
  78.3 1.0 pad_maximum_fusion.2.table_ref.refs_1_
  79.3 0.8 broadcast_in_dim.46.wave_ref.refs_2_
  80.1 18.0 %forward_fourier.6 = bf16[160,2,80,128]{3,2,1,0:T(8,128)(2,1)} custom-call(s32[80]{0:T(128)} %dynamic_slice.6.lon_ref, bf16[80,128,1280]{2,1,0:T(8,128)(2,1)} %reshape.81.grid_ref, bf16[320,1280]{1,0:T(8,128)(2,1)} %pad_maximum_fusion.2.table_ref.refs_1_, s32[320,128]{1,0:T(8,128)} %broadcast_in_dim.46.wave_ref.refs_2_), custom_call_target="tpu_custom_call" | custom-call | flops 8388608000 | bytes 32768000 | tf_op jit(solution)/shard_map/forward_fourier/pallas_call | solution.py:54
  98.0 122.0 %all-to-all-done.6.in_ref = bf16[32,5,2,80,128]{4,3,2,1,0:T(8,128)(2,1)} async-done(((bf16[32,5,2,80,128]{4,3,2,1,0:T(8,128)(2,1)}), bf16[32,5,2,80,128]{4,3,2,1,0:T(8,128)(2,1)}, u32[]{:S(2)}, u32[]{:S(2)}) %all-to-all-start.6) | async-done | bytes 6553632 | tf_op jit(solution)/shard_map/all_to_all | solution.py:243
  220.0 6.1 all-to-all-start.4
  226.3 3.7 multiply_convert_fusion.5
  230.1 1.0 pad_maximum_fusion.1.table_ref.refs_1_
  231.8 18.0 %forward_fourier.5 = bf16[160,2,80,128]{3,2,1,0:T(8,128)(2,1)} custom-call(s32[80]{0:T(128)} %dynamic_slice.6.lon_ref, bf16[80,128,1280]{2,1,0:T(8,128)(2,1)} %reshape.81.grid_ref, bf16[320,1280]{1,0:T(8,128)(2,1)} %pad_maximum_fusion.1.table_ref.refs_1_, s32[320,128]{1,0:T(8,128)} %broadcast_in_dim.44.wave_ref.refs_2_), custom_call_target="tpu_custom_call" | custom-call | flops 8388608000 | bytes 32768000 | tf_op jit(solution)/shard_map/forward_fourier/pallas_call | solution.py:54
  249.8 121.9 %all-to-all-done.4.in_ref = bf16[32,5,2,80,128]{4,3,2,1,0:T(8,128)(2,1)} async-done(((bf16[32,5,2,80,128]{4,3,2,1,0:T(8,128)(2,1)}), bf16[32,5,2,80,128]{4,3,2,1,0:T(8,128)(2,1)}, u32[]{:S(2)}, u32[]{:S(2)}) %all-to-all-start.4) | async-done | bytes 6553632 | tf_op jit(solution)/shard_map/all_to_all | solution.py:243
  371.7 6.3 all-to-all-start.2
  378.2 3.7 multiply_convert_fusion.7
  382.0 1.0 pad_maximum_fusion.table_ref.refs_1_
  382.9 0.8 broadcast_in_dim.41.wave_ref.refs_2_
  383.7 17.9 %forward_fourier.4 = bf16[160,2,80,128]{3,2,1,0:T(8,128)(2,1)} custom-call(s32[80]{0:T(128)} %dynamic_slice.6.lon_ref, bf16[80,128,1280]{2,1,0:T(8,128)(2,1)} %reshape.81.grid_ref, bf16[320,1280]{1,0:T(8,128)(2,1)} %pad_maximum_fusion.table_ref.refs_1_, s32[320,128]{1,0:T(8,128)} %broadcast_in_dim.41.wave_ref.refs_2_), custom_call_target="tpu_custom_call" | custom-call | flops 8388608000 | bytes 32768000 | tf_op jit(solution)/shard_map/forward_fourier/pallas_call | solution.py:54
  401.7 122.0 %all-to-all-done.2.in_ref = bf16[32,5,2,80,128]{4,3,2,1,0:T(8,128)(2,1)} async-done(((bf16[32,5,2,80,128]{4,3,2,1,0:T(8,128)(2,1)}), bf16[32,5,2,80,128]{4,3,2,1,0:T(8,128)(2,1)}, u32[]{:S(2)}, u32[]{:S(2)}) %all-to-all-start.2) | async-done | bytes 6553632 | tf_op jit(solution)/shard_map/all_to_all | solution.py:243
  523.6 6.1 all-to-all-start
  530.5 37.4 %all_gather.6 = bf16[128,128]{1,0:T(8,128)(2,1)S(1)} all-gather(bf16[32,128]{1,0:T(8,128)(2,1)S(1)} %copy-done), channel_id=1, replica_groups=mesh['lat'=8,'lev'=4] {'lev'}, dimensions={0}, use_global_device_ids=true | all-gather | bytes 40960 | tf_op jit(solution)/shard_map/all_gather | solution.py:224
  569.6 8.2 all-reduce
  578.0 6.2 broadcast_multiply_fusion
  584.2 33.2 %mul.178.mixer_ref = bf16[512,512]{1,0:T(8,128)(2,1)} reshape(bf16[128,4,128,4]{3,2,1,0:T(8,128)(2,1)} %broadcast_multiply_fusion) | data formatting | bytes 1048576 | tf_op jit(solution)/shard_map/jit(kron)/mul | solution.py:226
  618.1 1.3 add_divide_fusion.factor_ref
  619.4 18.8 %spectral_step.7 = bf16[32,5,2,80,128]{4,3,2,1,0:T(8,128)(2,1)} custom-call(s32[1]{0:T(128)} %bitcast.11.own_ref, s32[5]{0:T(128)} %get-tuple-element.17.wave_ref, bf16[80,640,640]{2,1,0:T(8,128)(2,1)} %table_ref.7, bf16[32,5,2,80,128]{4,3,2,1,0:T(8,128)(2,1)} %all-to-all-done.6.in_ref, bf16[512,512]{1,0:T(8,128)(2,1)} %mul.178.mixer_ref, ...), custom_call_target="tpu_custom_call" | custom-call | flops 11744051200 | bytes 17203200 | tf_op jit(solution)/shard_map/spectral_step/pallas_call | solution.py:113
  638.3 37.1 %all-to-all-done.in_ref = bf16[32,5,2,80,128]{4,3,2,1,0:T(8,128)(2,1)} async-done(((bf16[32,5,2,80,128]{4,3,2,1,0:T(8,128)(2,1)}), bf16[32,5,2,80,128]{4,3,2,1,0:T(8,128)(2,1)}, u32[]{:S(2)}, u32[]{:S(2)}) %all-to-all-start) | async-done | bytes 6553632 | tf_op jit(solution)/shard_map/all_to_all | solution.py:243
  675.4 6.1 all-to-all-start.7
  681.5 18.8 %spectral_step.6 = bf16[32,5,2,80,128]{4,3,2,1,0:T(8,128)(2,1)} custom-call(s32[1]{0:T(128)} %bitcast.8.own_ref, s32[5]{0:T(128)} %get-tuple-element.18.wave_ref, bf16[80,640,640]{2,1,0:T(8,128)(2,1)} %table_ref.7, bf16[32,5,2,80,128]{4,3,2,1,0:T(8,128)(2,1)} %all-to-all-done.4.in_ref, bf16[512,512]{1,0:T(8,128)(2,1)} %mul.178.mixer_ref, ...), custom_call_target="tpu_custom_call" | custom-call | flops 11744051200 | bytes 17203200 | tf_op jit(solution)/shard_map/spectral_step/pallas_call | solution.py:113
  700.3 126.8 %all-to-all-done.7 = bf16[32,5,2,80,128]{4,3,2,1,0:T(8,128)(2,1)} async-done(((bf16[32,5,2,80,128]{4,3,2,1,0:T(8,128)(2,1)}), bf16[32,5,2,80,128]{4,3,2,1,0:T(8,128)(2,1)}, u32[]{:S(2)}, u32[]{:S(2)}) %all-to-all-start.7) | async-done | bytes 6553632 | tf_op jit(solution)/shard_map/all_to_all | solution.py:254
  827.1 6.3 all-to-all-start.5
  833.4 18.9 %spectral_step.5 = bf16[32,5,2,80,128]{4,3,2,1,0:T(8,128)(2,1)} custom-call(s32[1]{0:T(128)} %bitcast.5.own_ref, s32[5]{0:T(128)} %get-tuple-element.19.wave_ref, bf16[80,640,640]{2,1,0:T(8,128)(2,1)} %table_ref.7, bf16[32,5,2,80,128]{4,3,2,1,0:T(8,128)(2,1)} %all-to-all-done.2.in_ref, bf16[512,512]{1,0:T(8,128)(2,1)} %mul.178.mixer_ref, ...), custom_call_target="tpu_custom_call" | custom-call | flops 11744051200 | bytes 17203200 | tf_op jit(solution)/shard_map/spectral_step/pallas_call | solution.py:113
  852.3 126.7 %all-to-all-done.5 = bf16[32,5,2,80,128]{4,3,2,1,0:T(8,128)(2,1)} async-done(((bf16[32,5,2,80,128]{4,3,2,1,0:T(8,128)(2,1)}), bf16[32,5,2,80,128]{4,3,2,1,0:T(8,128)(2,1)}, u32[]{:S(2)}, u32[]{:S(2)}) %all-to-all-start.5) | async-done | bytes 6553632 | tf_op jit(solution)/shard_map/all_to_all | solution.py:254
  979.1 6.1 all-to-all-start.3
  985.2 18.8 %spectral_step.4 = bf16[32,5,2,80,128]{4,3,2,1,0:T(8,128)(2,1)} custom-call(s32[1]{0:T(128)} %bitcast.own_ref, s32[5]{0:T(128)} %get-tuple-element.20.wave_ref, bf16[80,640,640]{2,1,0:T(8,128)(2,1)} %table_ref.7, bf16[32,5,2,80,128]{4,3,2,1,0:T(8,128)(2,1)} %all-to-all-done.in_ref, bf16[512,512]{1,0:T(8,128)(2,1)} %mul.178.mixer_ref, ...), custom_call_target="tpu_custom_call" | custom-call | flops 11744051200 | bytes 17203200 | tf_op jit(solution)/shard_map/spectral_step/pallas_call | solution.py:113
  1004.0 126.8 %all-to-all-done.3 = bf16[32,5,2,80,128]{4,3,2,1,0:T(8,128)(2,1)} async-done(((bf16[32,5,2,80,128]{4,3,2,1,0:T(8,128)(2,1)}), bf16[32,5,2,80,128]{4,3,2,1,0:T(8,128)(2,1)}, u32[]{:S(2)}, u32[]{:S(2)}) %all-to-all-start.3) | async-done | bytes 6553632 | tf_op jit(solution)/shard_map/all_to_all | solution.py:254
  1130.8 6.1 all-to-all-start.1
  1136.9 25.0 %inverse_fourier.4.refs_3_ = f32[80,128,1280]{2,1,0:T(8,128)} custom-call(s32[80]{0:T(128)} %dynamic_slice.6.lon_ref, bf16[160,2,80,128]{3,2,1,0:T(8,128)(2,1)} %bitcast.13.refs_0_, bf16[320,1280]{1,0:T(8,128)(2,1)} %pad_maximum_fusion.3.table_ref.refs_1_, s32[320,128]{1,0:T(8,128)} %broadcast_in_dim.48.wave_ref.refs_2_), custom_call_target="tpu_custom_call" | custom-call | flops 8388608000 | bytes 58982400 | tf_op jit(solution)/shard_map/inverse_fourier/pallas_call | solution.py:190
  1161.9 43.8 %inverse_fourier.5.refs_3_ = f32[80,128,1280]{2,1,0:T(8,128)} custom-call(s32[80]{0:T(128)} %dynamic_slice.6.lon_ref, bf16[160,2,80,128]{3,2,1,0:T(8,128)(2,1)} %bitcast.10.refs_0_, bf16[320,1280]{1,0:T(8,128)(2,1)} %pad_maximum_fusion.2.table_ref.refs_1_, s32[320,128]{1,0:T(8,128)} %broadcast_in_dim.46.wave_ref.refs_2_, f32[80,128,1280]{2,1,0:T(8,128)} %inverse_fourier.4.refs_3_), custom_call_target="tpu_custom_call" | custom-call | flops 8388608000 | bytes 58982400 | tf_op jit(solution)/shard_map/inverse_fourier/pallas_call | solution.py:190
  1205.7 43.9 %inverse_fourier.6.refs_3_ = f32[80,128,1280]{2,1,0:T(8,128)} custom-call(s32[80]{0:T(128)} %dynamic_slice.6.lon_ref, bf16[160,2,80,128]{3,2,1,0:T(8,128)(2,1)} %bitcast.7.refs_0_, bf16[320,1280]{1,0:T(8,128)(2,1)} %pad_maximum_fusion.1.table_ref.refs_1_, s32[320,128]{1,0:T(8,128)} %broadcast_in_dim.44.wave_ref.refs_2_, f32[80,128,1280]{2,1,0:T(8,128)} %inverse_fourier.5.refs_3_), custom_call_target="tpu_custom_call" | custom-call | flops 8388608000 | bytes 58982400 | tf_op jit(solution)/shard_map/inverse_fourier/pallas_call | solution.py:190
  1249.6 32.9 %all-to-all-done.1 = bf16[32,5,2,80,128]{4,3,2,1,0:T(8,128)(2,1)} async-done(((bf16[32,5,2,80,128]{4,3,2,1,0:T(8,128)(2,1)}), bf16[32,5,2,80,128]{4,3,2,1,0:T(8,128)(2,1)}, u32[]{:S(2)}, u32[]{:S(2)}) %all-to-all-start.1) | async-done | bytes 6553632 | tf_op jit(solution)/shard_map/all_to_all | solution.py:254
  1282.5 35.3 %inverse_fourier.7 = bf16[80,128,1280]{2,1,0:T(8,128)(2,1)} custom-call(s32[80]{0:T(128)} %dynamic_slice.6.lon_ref, bf16[160,2,80,128]{3,2,1,0:T(8,128)(2,1)} %bitcast.4.refs_0_, bf16[320,1280]{1,0:T(8,128)(2,1)} %pad_maximum_fusion.table_ref.refs_1_, s32[320,128]{1,0:T(8,128)} %broadcast_in_dim.41.wave_ref.refs_2_, f32[80,128,1280]{2,1,0:T(8,128)} %inverse_fourier.6.refs_3_), custom_call_target="tpu_custom_call" | custom-call | flops 8388608000 | bytes 58982400 | tf_op jit(solution)/shard_map/inverse_fourier/pallas_call | solution.py:190
  1317.9 42.9 %reshape.94 = bf16[80,32,4,1280]{3,2,1,0:T(4,128)(2,1)} reshape(bf16[80,128,1280]{2,1,0:T(8,128)(2,1)} %inverse_fourier.7) | data formatting | bytes 52428800 | tf_op jit(solution)/shard_map/reshape | solution.py:267
  (30 shorter events, 4.2 us)
Async XLA Ops:
  66.9 153.1 %all-to-all-start.6 = ((bf16[32,5,2,80,128]{4,3,2,1,0:T(8,128)(2,1)}), bf16[32,5,2,80,128]{4,3,2,1,0:T(8,128)(2,1)}, u32[]{:S(2)}, u32[]{:S(2)}) async-start(bf16[32,5,2,80,128]{4,3,2,1,0:T(8,128)(2,1)} %bitcast.19), calls=%async_computation.6 | async-start | bytes 13107200 | tf_op jit(solution)/shard_map/all_to_all | solution.py:243
  220.0 151.7 %all-to-all-start.4 = ((bf16[32,5,2,80,128]{4,3,2,1,0:T(8,128)(2,1)}), bf16[32,5,2,80,128]{4,3,2,1,0:T(8,128)(2,1)}, u32[]{:S(2)}, u32[]{:S(2)}) async-start(bf16[32,5,2,80,128]{4,3,2,1,0:T(8,128)(2,1)} %bitcast.18), calls=%async_computation.4 | async-start | bytes 13107200 | tf_op jit(solution)/shard_map/all_to_all | solution.py:243
  371.7 151.9 %all-to-all-start.2 = ((bf16[32,5,2,80,128]{4,3,2,1,0:T(8,128)(2,1)}), bf16[32,5,2,80,128]{4,3,2,1,0:T(8,128)(2,1)}, u32[]{:S(2)}, u32[]{:S(2)}) async-start(bf16[32,5,2,80,128]{4,3,2,1,0:T(8,128)(2,1)} %bitcast.17), calls=%async_computation.2 | async-start | bytes 13107200 | tf_op jit(solution)/shard_map/all_to_all | solution.py:243
  523.6 6.9 copy-start
  523.6 44.4 %copy-start.2 = (u32[32]{0:T(128)S(1)}, u32[32]{0:T(128)}, u32[]{:S(2)}) copy-start(u32[32]{0:T(128)} %constant.57) | copy-start | bytes 388
  523.6 45.7 %copy-start.1 = (bf16[32]{0:T(256)(128)(2,1)S(1)}, bf16[32]{0:T(256)(128)(2,1)}, u32[]{:S(2)}) copy-start(bf16[32]{0:T(256)(128)(2,1)} %param.9) | copy-start | bytes 196
  523.6 151.8 %all-to-all-start = ((bf16[32,5,2,80,128]{4,3,2,1,0:T(8,128)(2,1)}), bf16[32,5,2,80,128]{4,3,2,1,0:T(8,128)(2,1)}, u32[]{:S(2)}, u32[]{:S(2)}) async-start(bf16[32,5,2,80,128]{4,3,2,1,0:T(8,128)(2,1)} %bitcast.16), calls=%async_computation | async-start | bytes 13107200 | tf_op jit(solution)/shard_map/all_to_all | solution.py:243
  675.4 151.7 %all-to-all-start.7 = ((bf16[32,5,2,80,128]{4,3,2,1,0:T(8,128)(2,1)}), bf16[32,5,2,80,128]{4,3,2,1,0:T(8,128)(2,1)}, u32[]{:S(2)}, u32[]{:S(2)}) async-start(bf16[32,5,2,80,128]{4,3,2,1,0:T(8,128)(2,1)} %spectral_step.7), calls=%async_computation.7 | async-start | bytes 13107200 | tf_op jit(solution)/shard_map/all_to_all | solution.py:254
  827.1 151.9 %all-to-all-start.5 = ((bf16[32,5,2,80,128]{4,3,2,1,0:T(8,128)(2,1)}), bf16[32,5,2,80,128]{4,3,2,1,0:T(8,128)(2,1)}, u32[]{:S(2)}, u32[]{:S(2)}) async-start(bf16[32,5,2,80,128]{4,3,2,1,0:T(8,128)(2,1)} %spectral_step.6), calls=%async_computation.5 | async-start | bytes 13107200 | tf_op jit(solution)/shard_map/all_to_all | solution.py:254
  979.1 151.8 %all-to-all-start.3 = ((bf16[32,5,2,80,128]{4,3,2,1,0:T(8,128)(2,1)}), bf16[32,5,2,80,128]{4,3,2,1,0:T(8,128)(2,1)}, u32[]{:S(2)}, u32[]{:S(2)}) async-start(bf16[32,5,2,80,128]{4,3,2,1,0:T(8,128)(2,1)} %spectral_step.5), calls=%async_computation.3 | async-start | bytes 13107200 | tf_op jit(solution)/shard_map/all_to_all | solution.py:254
  1130.8 151.7 %all-to-all-start.1 = ((bf16[32,5,2,80,128]{4,3,2,1,0:T(8,128)(2,1)}), bf16[32,5,2,80,128]{4,3,2,1,0:T(8,128)(2,1)}, u32[]{:S(2)}, u32[]{:S(2)}) async-start(bf16[32,5,2,80,128]{4,3,2,1,0:T(8,128)(2,1)} %spectral_step.4), calls=%async_computation.1 | async-start | bytes 13107200 | tf_op jit(solution)/shard_map/all_to_all | solution.py:254
